TPU v7x, 512 devices: a whole 4x8x8 slice. The times are simulated.
512 devices in a mesh: section: 8 (over y), dp: 64 (over x, z, core).
Axes of the slice: x: 4, y: 8, z: 8, core: 2. Of those that a mesh axis runs over, the one named last changes fastest.
Arguments:
- activations: bfloat16 [8, 4, 64, 14336], P('section', None, 'dp'), may hold values from -6 to 6
- out_grads: bfloat16 [8, 4, 64, 4096], P('section', None, 'dp'), may hold values from -6 to 6
- basis_in: bfloat16 [8, 14336, 1024], P('section', 'dp'), may hold values from -0.046875 to 0.046875
- basis_out: bfloat16 [8, 4096, 1024], P('section', 'dp'), may hold values from -0.09375 to 0.09375
- eigen_values: float32 [8, 1024, 1024], P('section', 'dp'), may hold values from 0.02 to 2
- query_proj: bfloat16 [8, 8, 1024, 1024], P('section', None, 'dp'), may hold values from -0.046875 to 0.046875
- lengths: int32 [4], replicated, may hold values from 16 to 64
- seq_rows: int32 [4], replicated, may hold values from 0 to 511
- prior_table: float32 [512, 8], P('dp'), may hold values from -6 to 6
Outputs:
- influence: float32 [8, 512, 8], P('section', 'dp')
All inputs are finite; a program needn't handle non-finite values.
Results may differ from a plain program's by a relative error of at most 0.01.
Values may be sent and summed in bfloat16 or wider, within the bound.
A program may use at most 64 MiB of HBM per device.

v0:
```python
import jax
import jax.numpy as jnp
from jax import lax
from jax.sharding import PartitionSpec as P

DAMPING = 0.01


def in_blocks(value, dim, count):
    dims = value.shape
    blocks = value.reshape(*dims[:dim], count, dims[dim] // count, *dims[dim + 1 :])
    return jnp.moveaxis(blocks, dim, 0)


def sum_at_owner(value, axis, dim):
    blocks = in_blocks(value, dim, lax.axis_size(axis))
    arrived = lax.all_to_all(blocks, axis, split_axis=0, concat_axis=0, tiled=True)
    return arrived.astype(jnp.float32).sum(axis=0)


def copy_for_each(value, axis):
    count = lax.axis_size(axis)
    return lax.all_to_all(
        jnp.broadcast_to(value[None], (count, *value.shape)), axis, 0, 0, tiled=True
    )


def in_order(blocks, dim):
    dims = list(blocks.shape[1:])
    dims[dim] *= blocks.shape[0]
    return jnp.moveaxis(blocks, 0, dim).reshape(dims)


def gather_directly(value, axis, dim):
    blocks = copy_for_each(value, axis)
    return in_order(blocks, dim)


def of_everyone(value, axis):
    everything = copy_for_each(value, axis)
    return jnp.sum(everything, axis=0)


def folded_in_pairs(pieces, combine):
    while len(jax.tree.leaves(pieces)[0]) > 1:
        pieces = jax.vmap(combine)(*(pieces[side::2] for side in (0, 1)))
    return pieces[0]


def prefix(value, axis, combine, identity):
    count, position = (lax.axis_size(axis), lax.axis_index(axis))
    passed = jnp.arange(count) < position

    def kept(part, zero, own):
        part = jnp.where(
            passed.reshape(-1, *(1 for _ in own.shape)), part, jnp.asarray(zero, own.dtype)
        )
        return part

    pieces = copy_for_each(value, axis)
    return folded_in_pairs(kept(pieces, identity, value), combine)


def add_pair(earlier, latter):
    return earlier + latter


def per_device(
    activations,
    out_grads,
    basis_in,
    basis_out,
    eigen_values,
    query_proj,
    lengths,
    seq_rows,
    prior_table,
):
    micro = activations.shape[1]
    cols_acts, cols_grads = (
        lax.all_to_all(activations[0], "dp", split_axis=2, concat_axis=1, tiled=True),
        lax.all_to_all(out_grads[0], "dp", split_axis=2, concat_axis=1, tiled=True),
    )
    slots = cols_acts.shape[1]
    rank_size = basis_in.shape[2]
    act_part = jnp.dot(
        cols_acts.reshape(micro * slots, cols_acts.shape[2]),
        basis_in[0],
        preferred_element_type=jnp.float32,
    )
    grad_part = jnp.dot(
        cols_grads.reshape(micro * slots, cols_grads.shape[2]),
        basis_out[0],
        preferred_element_type=jnp.float32,
    )
    grad_share = sum_at_owner(grad_part.astype(jnp.bfloat16), "dp", 1).astype(jnp.bfloat16)
    act_share = sum_at_owner(act_part.astype(jnp.bfloat16), "dp", 1).astype(jnp.bfloat16)
    act_proj = gather_directly(act_share, "dp", 1)
    block_rows = grad_share.shape[1]
    position = jnp.arange(slots, dtype=jnp.int32)
    live_mask = (position[None, :] < lengths[:, None]).reshape(micro * slots, 1)
    grad_share = jnp.where(live_mask, grad_share, jnp.zeros_like(grad_share))
    inverse_len = 1.0 / lengths.astype(jnp.float32)
    seq_block = (
        jnp.einsum(
            "mti,mtj->mij",
            grad_share.reshape(micro, slots, block_rows),
            act_proj.reshape(micro, slots, rank_size),
            preferred_element_type=jnp.float32,
        )
        * inverse_len[:, None, None]
    )
    precond = (query_proj[0].astype(jnp.float32) / (eigen_values[0][None] + DAMPING)).astype(
        jnp.bfloat16
    )
    partial_value = jnp.einsum(
        "mij,qij->mq", seq_block, precond.astype(jnp.float32), precision=lax.Precision.HIGHEST
    )
    table_rows = prior_table.shape[0]
    first_row = lax.axis_index("dp") * table_rows
    summed = of_everyone(partial_value, "dp")
    before = prefix(summed, "section", add_pair, jnp.zeros_like(summed))
    owner_mask = (
        seq_rows[None, :] == (first_row + jnp.arange(table_rows, dtype=jnp.int32))[:, None]
    ).astype(jnp.float32)
    result = prior_table + jnp.dot(owner_mask, before + summed, precision=lax.Precision.HIGHEST)
    return result[None]


def solution(mesh):
    return jax.shard_map(
        per_device,
        mesh=mesh,
        in_specs=(
            P("section", None, "dp", None),
            P("section", None, "dp", None),
            P("section", "dp", None),
            P("section", "dp", None),
            P("section", "dp", None),
            P("section", None, "dp", None),
            P(),
            P(),
            P("dp", None),
        ),
        out_specs=P("section", "dp", None),
        check_vma=False,
    )
```

profile of v0, /device:TPU:56, one launch (start us, length us, event | category | flops | bytes accessed | tf_op | source)
XLA Modules:
  0.0 288.7 jit_solution(8253465935081749725)
XLA Ops:
  0.0 13.7 %copy.48 = bf16[4,1,14336]{0,1,2:T(2,128)(2,1)} copy(bf16[4,1,14336]{2,0,1:T(4,128)(2,1)} %bitcast.48) | data formatting | bytes 229376 | tf_op jit(solution)/shard_map/squeeze | solution.py:81
  14.2 79.8 %reduce.2 = bf16[14336,4]{1,0:T(8,128)(2,1)} reduce(bf16[14336,1,4]{2,1,0:T(2,128)(2,1)} %bitcast.44, bf16[]{:T(256)} %broadcast.27), dimensions={1}, to_apply=%bitcast.37.reduce_sub_computation | reduce | bytes 229378
  94.1 5.9 %reshape.62 = bf16[64,2,448]{2,1,0:T(2,128)(2,1)} reshape(bf16[14336,4]{1,0:T(8,128)(2,1)} %reduce.2) | data formatting | bytes 229376
  100.0 14.0 %all-to-all-start.2 = ((bf16[64,2,448]{2,1,0:T(2,128)(2,1)}), bf16[64,2,448]{2,1,0:T(2,128)(2,1)S(1)}, u32[]{:S(2)}, u32[]{:S(2)}) async-start(bf16[64,2,448]{2,1,0:T(2,128)(2,1)} %reshape.62), calls=%async_computation.2 | async-start | bytes 262144 | tf_op jit(solution)/shard_map/all_to_all | solution.py:81
  114.0 2.8 copy.44
  116.8 23.4 %reduce.3 = bf16[4096,4]{1,0:T(8,128)(2,1)} reduce(bf16[4096,1,4]{2,1,0:T(2,128)(2,1)S(1)} %bitcast.45, bf16[]{:T(256)} %broadcast.27), dimensions={1}, to_apply=%bitcast.39.reduce_sub_computation | reduce | bytes 65538
  140.2 3.7 %reshape.64 = bf16[64,2,128]{2,1,0:T(2,128)(2,1)} reshape(bf16[4096,4]{1,0:T(8,128)(2,1)} %reduce.3) | data formatting | bytes 65536
  143.9 10.2 %all-to-all-start = ((bf16[64,2,128]{2,1,0:T(2,128)(2,1)}), bf16[64,2,128]{2,1,0:T(2,128)(2,1)S(1)}, u32[]{:S(2)}, u32[]{:S(2)}) async-start(bf16[64,2,128]{2,1,0:T(2,128)(2,1)} %reshape.64), calls=%async_computation | async-start | bytes 65536 | tf_op jit(solution)/shard_map/all_to_all | solution.py:82
  154.1 11.0 %reshape.63 = bf16[14336,1,4]{2,1,0:T(2,128)(2,1)} reshape(bf16[64,2,448]{2,1,0:T(2,128)(2,1)S(1)} %all-to-all-done.2) | data formatting | bytes 229376
  165.1 13.9 %copy.49 = bf16[4,1,14336]{2,0,1:T(4,128)(2,1)S(1)} copy(bf16[4,1,14336]{0,1,2:T(2,128)(2,1)} %bitcast.43) | data formatting | bytes 229376 | tf_op jit(solution)/shard_map/all_to_all | solution.py:81
  179.5 1.0 copy.50
  180.5 10.3 %all-to-all-start.3 = ((bf16[64,256,16]{1,2,0:T(8,128)(2,1)}), bf16[64,256,16]{1,2,0:T(8,128)(2,1)S(1)}, u32[]{:S(2)}, u32[]{:S(2)}) async-start(bf16[64,256,16]{1,2,0:T(8,128)(2,1)} %bitcast.7), calls=%async_computation.3 | async-start | bytes 1048576 | tf_op jit(solution)/shard_map/all_to_all | solution.py:17
  190.9 2.8 reshape.65
  193.7 2.0 copy.45
  196.1 1.0 copy.46
  197.1 10.8 %all-to-all-done.3 = bf16[64,256,16]{1,2,0:T(8,128)(2,1)S(1)} async-done(((bf16[64,256,16]{1,2,0:T(8,128)(2,1)}), bf16[64,256,16]{1,2,0:T(8,128)(2,1)S(1)}, u32[]{:S(2)}, u32[]{:S(2)}) %all-to-all-start.3) | async-done | bytes 524320 | tf_op jit(solution)/shard_map/all_to_all | solution.py:17
  207.9 6.5 %all-to-all-start.1 = ((bf16[64,256,16]{1,2,0:T(8,128)(2,1)}), bf16[64,256,16]{1,2,0:T(8,128)(2,1)S(1)}, u32[]{:S(2)}, u32[]{:S(2)}) async-start(bf16[64,256,16]{1,2,0:T(8,128)(2,1)} %bitcast.3), calls=%async_computation.1 | async-start | bytes 1048576 | tf_op jit(solution)/shard_map/all_to_all | solution.py:17
  214.6 16.9 %all-to-all-done.1 = bf16[64,256,16]{1,2,0:T(8,128)(2,1)S(1)} async-done(((bf16[64,256,16]{1,2,0:T(8,128)(2,1)}), bf16[64,256,16]{1,2,0:T(8,128)(2,1)S(1)}, u32[]{:S(2)}, u32[]{:S(2)}) %all-to-all-start.1) | async-done | bytes 524320 | tf_op jit(solution)/shard_map/all_to_all | solution.py:17
  232.3 6.5 %all-to-all-start.4 = ((bf16[64,256,16]{1,2,0:T(8,128)(2,1)}), bf16[64,256,16]{1,2,0:T(8,128)(2,1)S(1)}, u32[]{:S(2)}, u32[]{:S(2)}) async-start(bf16[64,256,16]{1,2,0:T(8,128)(2,1)} %broadcast_in_dim.33), calls=%async_computation.4 | async-start | bytes 1048576 | tf_op jit(solution)/shard_map/all_to_all | solution.py:23
  239.2 16.7 %all-to-all-done.4 = bf16[64,256,16]{1,2,0:T(8,128)(2,1)S(1)} async-done(((bf16[64,256,16]{1,2,0:T(8,128)(2,1)}), bf16[64,256,16]{1,2,0:T(8,128)(2,1)S(1)}, u32[]{:S(2)}, u32[]{:S(2)}) %all-to-all-start.4) | async-done | bytes 524320 | tf_op jit(solution)/shard_map/all_to_all | solution.py:23
  258.4 6.5 %all-to-all-start.5 = ((f32[64,4,8]{2,1,0:T(4,128)}), f32[64,4,8]{2,1,0:T(4,128)S(1)}, u32[]{:S(2)}, u32[]{:S(2)}) async-start(f32[64,4,8]{2,1,0:T(4,128)} %broadcast_in_dim.54), calls=%async_computation.5 | async-start | bytes 262144 | tf_op jit(solution)/shard_map/all_to_all | solution.py:23
  264.9 10.3 %all-to-all-done.5 = f32[64,4,8]{2,1,0:T(4,128)S(1)} async-done(((f32[64,4,8]{2,1,0:T(4,128)}), f32[64,4,8]{2,1,0:T(4,128)S(1)}, u32[]{:S(2)}, u32[]{:S(2)}) %all-to-all-start.5) | async-done | bytes 8224 | tf_op jit(solution)/shard_map/all_to_all | solution.py:23
  275.9 6.9 %all-to-all-start.6 = ((f32[8,4,8]{2,1,0:T(4,128)}), f32[8,4,8]{2,1,0:T(4,128)S(1)}, u32[]{:S(2)}, u32[]{:S(2)}) async-start(f32[8,4,8]{2,1,0:T(4,128)} %broadcast_in_dim.55), calls=%async_computation.6 | async-start | bytes 32768 | tf_op jit(solution)/shard_map/all_to_all | solution.py:23
  282.7 5.1 %all-to-all-done.6 = f32[8,4,8]{2,1,0:T(4,128)S(1)} async-done(((f32[8,4,8]{2,1,0:T(4,128)}), f32[8,4,8]{2,1,0:T(4,128)S(1)}, u32[]{:S(2)}, u32[]{:S(2)}) %all-to-all-start.6) | async-done | bytes 1056 | tf_op jit(solution)/shard_map/all_to_all | solution.py:23
  (43 shorter events, 6.7 us)
Async XLA Ops:
  0.0 179.2 %copy-start = (bf16[1,224,1024]{2,1,0:T(8,128)(2,1)S(1)}, bf16[1,224,1024]{2,1,0:T(8,128)(2,1)}, u32[]{:S(2)}) copy-start(bf16[1,224,1024]{2,1,0:T(8,128)(2,1)} %param.11) | copy-start | bytes 1376260
  94.1 19.9 %copy-start.4 = (bf16[1,4,1,4096]{3,1,2,0:T(4,128)(2,1)S(1)}, bf16[1,4,1,4096]{3,1,2,0:T(4,128)(2,1)}, u32[]{:S(2)}) copy-start(bf16[1,4,1,4096]{3,1,2,0:T(4,128)(2,1)} %param.10) | copy-start | bytes 98308
  100.0 43.9 %all-to-all-start.2 = ((bf16[64,2,448]{2,1,0:T(2,128)(2,1)}), bf16[64,2,448]{2,1,0:T(2,128)(2,1)S(1)}, u32[]{:S(2)}, u32[]{:S(2)}) async-start(bf16[64,2,448]{2,1,0:T(2,128)(2,1)} %reshape.62), calls=%async_computation.2 | async-start | bytes 262144 | tf_op jit(solution)/shard_map/all_to_all | solution.py:81
  143.9 36.6 %all-to-all-start = ((bf16[64,2,128]{2,1,0:T(2,128)(2,1)}), bf16[64,2,128]{2,1,0:T(2,128)(2,1)S(1)}, u32[]{:S(2)}, u32[]{:S(2)}) async-start(bf16[64,2,128]{2,1,0:T(2,128)(2,1)} %reshape.64), calls=%async_computation | async-start | bytes 65536 | tf_op jit(solution)/shard_map/all_to_all | solution.py:82
  179.2 16.6 %copy-start.2 = (bf16[1,64,1024]{2,1,0:T(8,128)(2,1)S(1)}, bf16[1,64,1024]{2,1,0:T(8,128)(2,1)}, u32[]{:S(2)}) copy-start(bf16[1,64,1024]{2,1,0:T(8,128)(2,1)} %param.12) | copy-start | bytes 393220
  180.5 27.4 %all-to-all-start.3 = ((bf16[64,256,16]{1,2,0:T(8,128)(2,1)}), bf16[64,256,16]{1,2,0:T(8,128)(2,1)S(1)}, u32[]{:S(2)}, u32[]{:S(2)}) async-start(bf16[64,256,16]{1,2,0:T(8,128)(2,1)} %bitcast.7), calls=%async_computation.3 | async-start | bytes 1048576 | tf_op jit(solution)/shard_map/all_to_all | solution.py:17
  193.6 45.2 %copy-start.6 = (s32[4]{0:T(128)S(1)}, s32[4]{0:T(128)}, u32[]{:S(2)}) copy-start(s32[4]{0:T(128)} %param.15) | copy-start | bytes 52
  193.6 45.3 %copy-start.1 = (bf16[1,8,16,1024]{3,2,1,0:T(8,128)(2,1)S(1)}, bf16[1,8,16,1024]{3,2,1,0:T(8,128)(2,1)}, u32[]{:S(2)}) copy-start(bf16[1,8,16,1024]{3,2,1,0:T(8,128)(2,1)} %param.14) | copy-start | bytes 786436
  195.7 43.3 %copy-start.3 = (f32[1,16,1024]{2,1,0:T(8,128)S(1)}, f32[1,16,1024]{2,1,0:T(8,128)}, u32[]{:S(2)}) copy-start(f32[1,16,1024]{2,1,0:T(8,128)} %param.13) | copy-start | bytes 196612
  207.9 23.6 %all-to-all-start.1 = ((bf16[64,256,16]{1,2,0:T(8,128)(2,1)}), bf16[64,256,16]{1,2,0:T(8,128)(2,1)S(1)}, u32[]{:S(2)}, u32[]{:S(2)}) async-start(bf16[64,256,16]{1,2,0:T(8,128)(2,1)} %bitcast.3), calls=%async_computation.1 | async-start | bytes 1048576 | tf_op jit(solution)/shard_map/all_to_all | solution.py:17
  214.5 73.5 %copy-start.5 = (f32[8,8]{1,0:T(8,128)S(1)}, f32[8,8]{1,0:T(8,128)}, u32[]{:S(2)}) copy-start(f32[8,8]{1,0:T(8,128)} %param.17) | copy-start | bytes 772
  214.5 73.5 %copy-start.7 = (s32[4]{0:T(128)S(1)}, s32[4]{0:T(128)}, u32[]{:S(2)}) copy-start(s32[4]{0:T(128)} %param.16) | copy-start | bytes 52
  232.3 23.6 %all-to-all-start.4 = ((bf16[64,256,16]{1,2,0:T(8,128)(2,1)}), bf16[64,256,16]{1,2,0:T(8,128)(2,1)S(1)}, u32[]{:S(2)}, u32[]{:S(2)}) async-start(bf16[64,256,16]{1,2,0:T(8,128)(2,1)} %broadcast_in_dim.33), calls=%async_computation.4 | async-start | bytes 1048576 | tf_op jit(solution)/shard_map/all_to_all | solution.py:23
  258.4 16.8 %all-to-all-start.5 = ((f32[64,4,8]{2,1,0:T(4,128)}), f32[64,4,8]{2,1,0:T(4,128)S(1)}, u32[]{:S(2)}, u32[]{:S(2)}) async-start(f32[64,4,8]{2,1,0:T(4,128)} %broadcast_in_dim.54), calls=%async_computation.5 | async-start | bytes 262144 | tf_op jit(solution)/shard_map/all_to_all | solution.py:23
  275.9 12.0 %all-to-all-start.6 = ((f32[8,4,8]{2,1,0:T(4,128)}), f32[8,4,8]{2,1,0:T(4,128)S(1)}, u32[]{:S(2)}, u32[]{:S(2)}) async-start(f32[8,4,8]{2,1,0:T(4,128)} %broadcast_in_dim.55), calls=%async_computation.6 | async-start | bytes 32768 | tf_op jit(solution)/shard_map/all_to_all | solution.py:23
where the time goes:
time: 293 us; the launch traced here: 289 us
  other arithmetic  104 us (35%)
  local copies, waits for them, and re-layouts  61.4 us (21%)
  starting transfers between devices  60.9 us (21%)
  waiting for transfers between devices  59.7 us (20%)
    unnamed x2, other arithmetic  103 us
    all_to_all x3, waiting for transfers between devices, copy_for_each(): lax.all_to_all(jnp.broadcast_to(value[None], (count, *value.shape)), axis...  32 us
    all_to_all x2, waiting for transfers between devices, sum_at_owner(): lax.all_to_all(blocks, axis, split_axis=0, concat_axis=0, tiled=True)  27.7 us
    unnamed x21, local copies, waits for them, and re-layouts  24 us
    all_to_all x3, starting transfers between devices, copy_for_each(): lax.all_to_all(jnp.broadcast_to(value[None], (count, *value.shape)), axis...  19.9 us
    all_to_all x2, starting transfers between devices, sum_at_owner(): lax.all_to_all(blocks, axis, split_axis=0, concat_axis=0, tiled=True)  16.8 us
    all_to_all x1, starting transfers between devices, per_device(): lax.all_to_all(activations[0], 'dp', split_axis=2, concat_axis=1, tiled=T...  14 us
    all_to_all x1, local copies, waits for them, and re-layouts, per_device(): lax.all_to_all(activations[0], 'dp', split_axis=2, concat_axis=1, tiled=T...  13.9 us
  transfers between devices with their start and end apart: 7, of which 5 were waited for; matrix products, arithmetic and copies ran while one was open for 22% of the time, Pallas kernels for 0%

commit v1 on v0

v1 whole, which is shorter than its diff:
```python
import functools

import jax
import jax.numpy as jnp
from jax import lax
from jax.experimental import pallas as pl
from jax.experimental.pallas import tpu as pltpu
from jax.sharding import PartitionSpec as P

DAMPING = 0.01
MESH = pl.DeviceIdType.MESH
NX = 4
NC = 2
KA = 224
KG = 64
WIN = 512
HIGH = lax.Precision.HIGHEST


def far_first(n):
    return sorted(range(1, n), key=lambda k: -min(k, n - k))


def kernel(
    n_sections,
    nz,
    a_hbm,
    g_hbm,
    b_hbm,
    w_hbm,
    e_hbm,
    q_hbm,
    len_ref,
    rows_ref,
    prior_ref,
    out_ref,
    a_v,
    g_v,
    e_v,
    q_v,
    b_full,
    w_full,
    w_t,
    p_send,
    p_full,
    x_recv,
    z_send,
    tok,
    xs_a,
    xs_g,
    xr_a,
    xr_g,
    zs_a,
    zs_g,
    zr_a,
    zr_g,
    ap_own,
    gp_own,
    ap_full,
    gp_full,
    rows_x,
    s1_send,
    s1_recv,
    s2_send,
    s2_recv,
    s3_send,
    s3_recv,
    load_sem,
    x_ss,
    x_rs,
    z_ss,
    z_rs,
    c_ss,
    c_rs,
    bw_ss,
    bw_rs,
    p_ss,
    p_rs,
    rx_ss,
    rx_rs,
    rz_ss,
    rz_rs,
    az_ss,
    az_rs,
    gx_ss,
    gx_rs,
    s1_ss,
    s1_rs,
    s2_ss,
    s2_rs,
    s3_ss,
    s3_rs,
):
    sec = lax.axis_index("section")
    dp = lax.axis_index("dp")
    x = dp // (2 * nz)
    z = (dp % (2 * nz)) // 2
    c = dp % 2
    ib = gp_own.shape[0]
    tz = ap_own.shape[0]
    half = w_full.shape[1]
    kx = x_recv.shape[2] - nz * 2 * KG
    kgx = nz * 2 * KG

    def at(xx, zz, cc):
        return (sec, (xx * nz + zz) * 2 + cc)

    def send(src, dst, ss, rs, dev):
        copy = pltpu.make_async_remote_copy(
            src_ref=src, dst_ref=dst, send_sem=ss, recv_sem=rs, device_id=dev, device_id_type=MESH
        )
        copy.start()
        pending.append(copy)

    def arrived(dst, ss, rs):
        pltpu.make_async_remote_copy(
            src_ref=dst,
            dst_ref=dst,
            send_sem=ss,
            recv_sem=rs,
            device_id=(sec, dp),
            device_id_type=MESH,
        ).wait_recv()

    pending = []
    far_x = far_first(NX)
    far_z = far_first(nz)
    far_s = far_first(n_sections)
    group = [(dx, dc) for dx in (2, 1, 3, 0) for dc in (0, 1) if dx or dc]

    off = pl.multiple_of(64 * (z % 2) + KA * c, 32)
    goff = pl.multiple_of(KG * c, 64)
    mine = pl.ds(pl.multiple_of(half * c, 128), half)
    other = pl.ds(pl.multiple_of(half * (1 - c), 128), half)
    a_own = a_hbm.at[:, pl.ds(pl.multiple_of(kx * x, 128), kx)]
    g_own = g_hbm.at[:, pl.ds(pl.multiple_of(kgx * x, 128), kgx)]
    loads = [
        pltpu.make_async_copy(s, d, load_sem.at[i])
        for i, (s, d) in enumerate(
            (
                (a_hbm, a_v),
                (g_hbm, g_v),
                (a_own, x_recv.at[x, :, pl.ds(0, kx)]),
                (g_own, x_recv.at[x, :, pl.ds(kx, kgx)]),
                (e_hbm, e_v),
                (q_hbm, q_v),
                (b_hbm.at[:, mine], b_full.at[pl.ds(off, KA), :]),
                (w_hbm.at[:, mine], w_full.at[pl.ds(goff, KG), :]),
            )
        )
    ]
    for load in loads:
        load.start()

    barrier = pltpu.get_barrier_semaphore()
    partners = [at(x, (z + k) % nz, c) for k in far_z]
    partners += [((sec + k) % n_sections, dp) for k in far_s]
    partners += [at((x + dx) % NX, z, (c + dc) % 2) for dx, dc in group]
    for dev in partners:
        pl.semaphore_signal(barrier, inc=1, device_id=dev, device_id_type=MESH)
    pl.semaphore_wait(barrier, len(partners))

    loads[0].wait()
    loads[1].wait()
    for k in far_x:
        xx = (x + k) % NX
        dev = at(xx, z, c)
        send(
            a_v.at[:, pl.ds(pl.multiple_of(kx * xx, 128), kx)],
            x_recv.at[x, :, pl.ds(0, kx)],
            x_ss.at[0, k],
            x_rs.at[0, k],
            dev,
        )
        send(
            g_v.at[:, pl.ds(pl.multiple_of(kgx * xx, 128), kgx)],
            x_recv.at[x, :, pl.ds(kx, kgx)],
            x_ss.at[1, k],
            x_rs.at[1, k],
            dev,
        )
    twin = at(x, z, 1 - c)
    send(b_hbm.at[:, other], b_full.at[pl.ds(off, KA), :], bw_ss.at[0], bw_rs.at[0], twin)
    send(w_hbm.at[:, other], w_full.at[pl.ds(goff, KG), :], bw_ss.at[1], bw_rs.at[1], twin)

    zero_at = pl.multiple_of((1 - z % 2) * 2 * KA, 64)
    b_full[pl.ds(zero_at, 64), :] = jnp.zeros((64, half), jnp.bfloat16)
    rows_x[...] = jnp.zeros_like(rows_x)
    loads[4].wait()
    loads[5].wait()
    for b in range(2 * NX):
        cols = slice(128 * b, 128 * b + 128)
        den = e_v[:, cols] + DAMPING
        num = q_v[:, :, cols].astype(jnp.float32)
        p_send[b] = (num / den[None]).astype(jnp.bfloat16)
    for i, (dx, dc) in enumerate(group):
        xx, cc = (x + dx) % NX, (c + dc) % 2
        send(
            p_send.at[4 * cc + xx],
            p_full.at[2 * x + c],
            p_ss.at[i],
            p_rs.at[i],
            at(xx, z, cc),
        )
    p_full[2 * x + c] = p_send[4 * c + x]

    loads[2].wait()
    loads[3].wait()
    for k in far_x:
        xx = (x + NX - k) % NX
        arrived(x_recv.at[xx, :, pl.ds(0, kx)], x_ss.at[0, k], x_rs.at[0, k])
        arrived(x_recv.at[xx, :, pl.ds(kx, kgx)], x_ss.at[1, k], x_rs.at[1, k])
    for zz in range(nz):
        start = 896 * (zz // 2) + 384 * (zz % 2)
        z_send[zz, :, 0:WIN] = jnp.concatenate(
            [x_recv[i, :, start : start + WIN] for i in range(NX)], axis=0
        )
        gs = kx + 2 * KG * zz
        z_send[zz, :, WIN : WIN + 2 * KG] = jnp.concatenate(
            [x_recv[i, :, gs : gs + 2 * KG] for i in range(NX)], axis=0
        )
    for k in far_z:
        zz = (z + k) % nz
        send(z_send.at[zz], tok.at[c, z], z_ss.at[k], z_rs.at[k], at(x, zz, c))
    send(z_send.at[z], tok.at[c, z], c_ss.at[0], c_rs.at[0], twin)
    tok[c, z] = z_send[z]

    loads[6].wait()
    loads[7].wait()
    arrived(w_full.at[pl.ds(pl.multiple_of(KG * (1 - c), 64), KG), :], bw_ss.at[1], bw_rs.at[1])
    w_t[...] = w_full[...].astype(jnp.float32).T.astype(jnp.bfloat16)
    off_twin = pl.multiple_of(64 * (z % 2) + KA * (1 - c), 32)
    arrived(b_full.at[pl.ds(off_twin, KA), :], bw_ss.at[0], bw_rs.at[0])

    for k in reversed(far_z):
        zz = (z + nz - k) % nz
        arrived(tok.at[c, zz], z_ss.at[k], z_rs.at[k])
        send(tok.at[c, zz], tok.at[c, zz], c_ss.at[k], c_rs.at[k], twin)
    arrived(tok.at[1 - c, z], c_ss.at[0], c_rs.at[0])
    for k in reversed(far_z):
        zz = (z + nz - k) % nz
        arrived(tok.at[1 - c, zz], c_ss.at[k], c_rs.at[k])

    tokens = 2 * nz * 16
    grads = tok[:, :, :, WIN : WIN + 2 * KG].reshape(tokens, 2 * KG)
    part_g = lax.dot_general(
        w_t[...], grads, (((1,), (1,)), ((), ())), preferred_element_type=jnp.float32
    ).astype(jnp.bfloat16)
    for i in range(NX):
        for zz in range(nz):
            r = (i // 2) * 2 * nz * ib + zz * 2 * ib + (i % 2) * ib
            xs_g[i, zz] = part_g[r : r + ib, :]
    for k in far_x:
        xx = (x + k) % NX
        send(xs_g.at[xx], xr_g.at[x], rx_ss.at[1, k], rx_rs.at[1, k], at(xx, z, c))
    acts = tok[:, :, :, 0:WIN].reshape(tokens, WIN)
    for i in range(NX):
        xs_a[i] = jnp.dot(
            acts, b_full[:, 128 * i : 128 * i + 128], preferred_element_type=jnp.float32
        ).astype(jnp.bfloat16)
    for k in far_x:
        xx = (x + k) % NX
        send(xs_a.at[xx], xr_a.at[x], rx_ss.at[0, k], rx_rs.at[0, k], at(xx, z, c))

    total = xs_g[x].astype(jnp.float32)
    for k in reversed(far_x):
        xx = (x + NX - k) % NX
        arrived(xr_g.at[xx], rx_ss.at[1, k], rx_rs.at[1, k])
        total = total + xr_g[xx].astype(jnp.float32)
    zs_g[...] = total.astype(jnp.bfloat16)
    for k in far_z:
        zz = (z + k) % nz
        send(zs_g.at[zz], zr_g.at[z], rz_ss.at[1, k], rz_rs.at[1, k], at(x, zz, c))
    total = xs_a[x].astype(jnp.float32)
    for k in reversed(far_x):
        xx = (x + NX - k) % NX
        arrived(xr_a.at[xx], rx_ss.at[0, k], rx_rs.at[0, k])
        total = total + xr_a[xx].astype(jnp.float32)
    zs_a[...] = total.astype(jnp.bfloat16).reshape(nz, tz, 128)
    for k in far_z:
        zz = (z + k) % nz
        send(zs_a.at[zz], zr_a.at[z], rz_ss.at[0, k], rz_rs.at[0, k], at(x, zz, c))

    total = zs_g[z].astype(jnp.float32)
    for k in reversed(far_z):
        zz = (z + nz - k) % nz
        arrived(zr_g.at[zz], rz_ss.at[1, k], rz_rs.at[1, k])
        total = total + zr_g[zz].astype(jnp.float32)
    gp_own[...] = total.astype(jnp.bfloat16)
    for i, (dx, dc) in enumerate(group):
        xx, cc = (x + dx) % NX, (c + dc) % 2
        send(gp_own, gp_full.at[4 * c + x], gx_ss.at[i], gx_rs.at[i], at(xx, z, cc))
    gp_full[4 * c + x] = total.astype(jnp.bfloat16)
    total = zs_a[z].astype(jnp.float32)
    for k in reversed(far_z):
        zz = (z + nz - k) % nz
        arrived(zr_a.at[zz], rz_ss.at[0, k], rz_rs.at[0, k])
        total = total + zr_a[zz].astype(jnp.float32)
    ap_own[...] = total.astype(jnp.bfloat16)
    for k in far_z:
        zz = (z + k) % nz
        send(ap_own, ap_full.at[z], az_ss.at[k], az_rs.at[k], at(x, zz, c))
    ap_full[z] = total.astype(jnp.bfloat16)

    for i, (dx, dc) in enumerate(group):
        xx, cc = (x + NX - dx) % NX, (c + 2 - dc) % 2
        arrived(p_full.at[2 * xx + cc], p_ss.at[i], p_rs.at[i])
        arrived(gp_full.at[4 * cc + xx], gx_ss.at[i], gx_rs.at[i])
    for k in reversed(far_z):
        zz = (z + nz - k) % nz
        arrived(ap_full.at[zz], az_ss.at[k], az_rs.at[k])
    lane = lax.broadcasted_iota(jnp.int32, (8 * ib, tokens), 1)
    micro = lane % 4
    slot = ((lane // 4) % 4) * 2 * nz + ((lane // 16) % nz) * 2 + lane // (16 * nz)
    gp = gp_full[...].reshape(8 * ib, tokens).astype(jnp.float32)
    ap = ap_full[...].reshape(tokens, 128)
    for m in range(4):
        live = jnp.where(micro == m, slot, 2**20) < len_ref[m]
        seq = jnp.dot(
            jnp.where(live, gp, 0.0).astype(jnp.bfloat16), ap, preferred_element_type=jnp.float32
        )
        for q in range(8):
            row = seq * p_full[:, q].reshape(8 * ib, 128).astype(jnp.float32)
            rows_x[m * 8 + q : m * 8 + q + 1, :] = jnp.sum(row, axis=0, keepdims=True)
    score = lax.dot_general(
        jnp.ones((8, 128), jnp.float32),
        rows_x[...],
        (((1,), (1,)), ((), ())),
        precision=HIGH,
        preferred_element_type=jnp.float32,
    )
    s1_send[...] = score[0:1, :]
    for i, (dx, dc) in enumerate(group):
        xx, cc = (x + dx) % NX, (c + dc) % 2
        send(s1_send, s1_recv.at[i], s1_ss.at[i], s1_rs.at[i], at(xx, z, cc))
    acc = score[0:1, :]
    for i, (dx, dc) in enumerate(group):
        arrived(s1_recv.at[i], s1_ss.at[i], s1_rs.at[i])
        acc = acc + s1_recv[i]
    s2_send[...] = acc
    for k in far_z:
        send(s2_send, s2_recv.at[k], s2_ss.at[k], s2_rs.at[k], at(x, (z + k) % nz, c))
    for k in reversed(far_z):
        arrived(s2_recv.at[k], s2_ss.at[k], s2_rs.at[k])
        acc = acc + s2_recv[k]
    s3_send[...] = acc
    for k in far_s:
        dev = ((sec + k) % n_sections, dp)
        send(s3_send, s3_recv.at[k], s3_ss.at[k], s3_rs.at[k], dev)
    for k in reversed(far_s):
        arrived(s3_recv.at[k], s3_ss.at[k], s3_rs.at[k])
        acc = acc + jnp.where(sec >= k, s3_recv[k], 0.0)

    lane = lax.broadcasted_iota(jnp.int32, (8, 128), 1)
    row = lax.broadcasted_iota(jnp.int32, (8, 128), 0) + dp * 8
    length = jnp.full((8, 128), 1, jnp.int32)
    target = jnp.full((8, 128), -1, jnp.int32)
    for m in range(4):
        inside = lane // 8 == m
        length = jnp.where(inside, len_ref[m], length)
        target = jnp.where(inside, rows_ref[m], target)
    scaled = acc * (1.0 / length.astype(jnp.float32))
    spread = jnp.where(target == row, scaled, 0.0)
    pick = lax.broadcasted_iota(jnp.int32, (128, 128), 0) % 8
    pick = pick == lax.broadcasted_iota(jnp.int32, (128, 128), 1)
    table = jnp.dot(
        spread, pick.astype(jnp.float32), precision=HIGH, preferred_element_type=jnp.float32
    )
    out_ref[...] = prior_ref[...] + table[:, 0:8]
    for copy in pending:
        copy.wait_send()


def per_device(n_sections, nz, acts, grads, basis_in, basis_out, eig, query, lengths, rows, prior):
    ff, d = acts.shape[3], grads.shape[3]
    rank = basis_in.shape[2]
    half = rank // 2
    ib = eig.shape[1]
    tokens = 2 * nz * 16
    tz = tokens // nz
    kx, kgx = ff // NX, d // NX
    bf, f32 = jnp.bfloat16, jnp.float32
    dma = pltpu.SemaphoreType.DMA
    vm = pltpu.VMEM
    hbm = pl.BlockSpec(memory_space=pl.ANY)
    smem = pl.BlockSpec(memory_space=pltpu.SMEM)
    vmem = pl.BlockSpec(memory_space=pltpu.VMEM)
    out = pl.pallas_call(
        functools.partial(kernel, n_sections, nz),
        out_shape=jax.ShapeDtypeStruct(prior.shape, f32),
        in_specs=[hbm] * 6 + [smem] * 2 + [vmem],
        out_specs=vmem,
        scratch_shapes=[
            vm((4, ff), bf),
            vm((4, d), bf),
            vm((ib, rank), f32),
            vm((8, ib, rank), bf),
            vm((WIN, half), bf),
            vm((2 * KG, half), bf),
            vm((half, 2 * KG), bf),
            vm((2 * NX, 8, ib, 128), bf),
            vm((2 * NX, 8, ib, 128), bf),
            vm((NX, 4, kx + kgx), bf),
            vm((nz, 16, WIN + 2 * KG), bf),
            vm((2, nz, 16, WIN + 2 * KG), bf),
            vm((NX, tokens, 128), bf),
            vm((NX, nz, ib, tokens), bf),
            vm((NX, tokens, 128), bf),
            vm((NX, nz, ib, tokens), bf),
            vm((nz, tz, 128), bf),
            vm((nz, ib, tokens), bf),
            vm((nz, tz, 128), bf),
            vm((nz, ib, tokens), bf),
            vm((tz, 128), bf),
            vm((ib, tokens), bf),
            vm((nz, tz, 128), bf),
            vm((2 * NX, ib, tokens), bf),
            vm((128, 128), f32),
            vm((1, 128), f32),
            vm((2 * NX, 1, 128), f32),
            vm((1, 128), f32),
            vm((nz, 1, 128), f32),
            vm((1, 128), f32),
            vm((n_sections, 1, 128), f32),
            dma((8,)),
            dma((2, NX)),
            dma((2, NX)),
            dma((nz,)),
            dma((nz,)),
            dma((nz,)),
            dma((nz,)),
            dma((2,)),
            dma((2,)),
            dma((7,)),
            dma((7,)),
            dma((2, NX)),
            dma((2, NX)),
            dma((2, nz)),
            dma((2, nz)),
            dma((nz,)),
            dma((nz,)),
            dma((7,)),
            dma((7,)),
            dma((7,)),
            dma((7,)),
            dma((nz,)),
            dma((nz,)),
            dma((n_sections,)),
            dma((n_sections,)),
        ],
        compiler_params=pltpu.CompilerParams(collective_id=0, has_side_effects=True),
    )(
        acts.reshape(4, ff),
        grads.reshape(4, d),
        basis_in[0],
        basis_out[0],
        eig[0],
        query[0],
        lengths,
        rows,
        prior,
    )
    return out[None]


def solution(mesh):
    n_sections, n_dp = mesh.shape["section"], mesh.shape["dp"]
    return jax.shard_map(
        functools.partial(per_device, n_sections, n_dp // (NX * NC)),
        mesh=mesh,
        in_specs=(
            P("section", None, "dp", None),
            P("section", None, "dp", None),
            P("section", "dp", None),
            P("section", "dp", None),
            P("section", "dp", None),
            P("section", None, "dp", None),
            P(),
            P(),
            P("dp", None),
        ),
        out_specs=P("section", "dp", None),
        check_vma=False,
    )
```

time: 293 us -> 60.1 us (0.21)
  the two profiles are of different devices: /device:TPU:56 before, /device:TPU:2 now
where the time goes in v1:
time: 60.1 us; the launch traced here: 60 us
  Pallas kernels  58.7 us (98%)
  local copies, waits for them, and re-layouts  1.28 us (2%)
    pallas_call x1, Pallas kernels, per_device(): pl.pallas_call(functools.partial(kernel, n_sections, nz), out_shape=jax.S...  58.7 us
    unnamed x1, local copies, waits for them, and re-layouts  1.28 us

profile of v1, /device:TPU:2, one launch (start us, length us, event | category | flops | bytes accessed | tf_op | source)
XLA Modules:
  0.0 60.0 jit_solution(17027410634193634534)
XLA Ops:
  0.0 58.7 %shard_map.91 = f32[8,8]{1,0:T(8,128)} custom-call(bf16[4,14336]{1,0:T(4,128)(2,1)} %bitcast.10, bf16[4,4096]{1,0:T(4,128)(2,1)} %bitcast.12, bf16[224,1024]{1,0:T(8,128)(2,1)} %bitcast.7, bf16[64,1024]{1,0:T(8,128)(2,1)} %bitcast.9, f32[16,1024]{1,0:T(8,128)} %bitcast.11, bf16[8,16,1024]{2,1,0:T(8,128)(2,1)} %bitcast.8, s32[4]{0:T(128)} %len_ref.1, ...), custom_call_target="tpu_custom_call" | custom-call | tf_op jit(solution)/shard_map/pallas_call | solution.py:388
  58.7 1.3 %copy.11 = f32[1,8,8]{2,1,0:T(8,128)} copy(f32[1,8,8]{2,1,0:T(8,128)} %bitcast.13) | data formatting | bytes 512

commit v2 on v1

v2 whole, which is shorter than its diff:
```python
import functools

import jax
import jax.numpy as jnp
from jax import lax
from jax.experimental import pallas as pl
from jax.experimental.pallas import tpu as pltpu
from jax.sharding import PartitionSpec as P

DAMPING = 0.01
MESH = pl.DeviceIdType.MESH
NX = 4
NC = 2
KA = 224
KG = 64
WIN = 512
SEMS = ("x", "z", "c", "bw", "p", "rx", "rz", "az", "gx", "s1", "s2", "s3")
HIGH = lax.Precision.HIGHEST


def far_first(n):
    return sorted(range(1, n), key=lambda k: -min(k, n - k))


def kernel(
    n_sections,
    nz,
    a_hbm,
    g_hbm,
    b_hbm,
    w_hbm,
    e_hbm,
    q_hbm,
    len_hbm,
    rows_hbm,
    prior_hbm,
    out_ref,
    len_ref,
    rows_ref,
    prior_ref,
    a_v,
    g_v,
    e_v,
    q_v,
    b_full,
    w_full,
    w_t,
    p_send,
    p_full,
    x_recv,
    z_send_a,
    z_send_g,
    tok_a,
    tok_g,
    xs_a,
    xs_g,
    xr_a,
    xr_g,
    zs_a,
    zs_g,
    zr_a,
    zr_g,
    ap_own,
    gp_own,
    ap_full,
    gp_full,
    rows_x,
    s1_send,
    s1_recv,
    s2_send,
    s2_recv,
    s3_send,
    s3_recv,
    load_sem,
    ready,
    *sem_refs,
):
    sec = lax.axis_index("section")
    dp = lax.axis_index("dp")
    x = dp // (2 * nz)
    z = (dp % (2 * nz)) // 2
    c = dp % 2
    ib = gp_own.shape[0]
    tz = ap_own.shape[0]
    half = w_full.shape[1]
    kgx = nz * 2 * KG
    kx = x_recv.shape[2] - kgx
    sems = dict(zip(SEMS, sem_refs, strict=True))

    def at(xx, zz, cc):
        return (sec, (xx * nz + zz) * 2 + cc)

    def copy_of(src, dst, name, i, dev):
        return pltpu.make_async_remote_copy(
            src_ref=src,
            dst_ref=dst,
            send_sem=sems[name].at[(0, *i)],
            recv_sem=sems[name].at[(1, *i)],
            device_id=dev,
            device_id_type=MESH,
        )

    def send(src, dst, name, i, dev):
        copy = copy_of(src, dst, name, i, dev)
        copy.start()
        pending.append(copy)

    def arrived(dst, name, i):
        copy_of(dst, dst, name, i, (sec, dp)).wait_recv()

    pending = []
    far_x = far_first(NX)
    far_z = far_first(nz)
    near_z = far_z[::-1]
    far_s = far_first(n_sections)
    group = [(dx, dc) for dx in (2, 1, 3, 0) for dc in (0, 1) if dx or dc]

    barrier = pltpu.get_barrier_semaphore()
    partners = [at((x + dx) % NX, z, (c + dc) % 2) for dx, dc in group]
    partners += [at(x, (z + k) % nz, c) for k in far_z]
    for dev in partners:
        pl.semaphore_signal(barrier, inc=1, device_id=dev, device_id_type=MESH)
    for k in far_s:

        @pl.when(sec + k < n_sections)
        def _(k=k):
            pl.semaphore_signal(barrier, inc=1, device_id=(sec + k, dp), device_id_type=MESH)

    off = pl.multiple_of(64 * (z % 2) + KA * c, 32)
    off_twin = pl.multiple_of(64 * (z % 2) + KA * (1 - c), 32)
    goff = pl.multiple_of(KG * c, 64)
    goff_twin = pl.multiple_of(KG * (1 - c), 64)
    mine = pl.ds(pl.multiple_of(half * c, 128), half)
    other = pl.ds(pl.multiple_of(half * (1 - c), 128), half)
    a_own = a_hbm.at[:, pl.ds(pl.multiple_of(kx * x, 128), kx)]
    g_own = g_hbm.at[:, pl.ds(pl.multiple_of(kgx * x, 128), kgx)]
    loads = [
        pltpu.make_async_copy(s, d, load_sem.at[i])
        for i, (s, d) in enumerate(
            (
                (g_hbm, g_v),
                (a_hbm, a_v),
                (g_own, x_recv.at[x, :, pl.ds(kx, kgx)]),
                (a_own, x_recv.at[x, :, pl.ds(0, kx)]),
                (e_hbm, e_v),
                (q_hbm, q_v),
                (b_hbm.at[:, mine], b_full.at[pl.ds(off, KA), :]),
                (w_hbm.at[:, mine], w_full.at[pl.ds(goff, KG), :]),
                (len_hbm, len_ref),
                (rows_hbm, rows_ref),
                (prior_hbm, prior_ref),
            )
        )
    ]
    for load in loads:
        load.start()

    pl.semaphore_wait(barrier, len(partners) + sec)

    loads[0].wait()
    for k in far_x:
        xx = (x + k) % NX
        send(
            g_v.at[:, pl.ds(pl.multiple_of(kgx * xx, 128), kgx)],
            x_recv.at[x, :, pl.ds(kx, kgx)],
            "x",
            (1, k),
            at(xx, z, c),
        )
    loads[1].wait()
    for k in far_x:
        xx = (x + k) % NX
        send(
            a_v.at[:, pl.ds(pl.multiple_of(kx * xx, 128), kx)],
            x_recv.at[x, :, pl.ds(0, kx)],
            "x",
            (0, k),
            at(xx, z, c),
        )
    twin = at(x, z, 1 - c)
    send(b_hbm.at[:, other], b_full.at[pl.ds(off, KA), :], "bw", (0,), twin)
    send(w_hbm.at[:, other], w_full.at[pl.ds(goff, KG), :], "bw", (1,), twin)

    zero_at = pl.multiple_of((1 - z % 2) * 2 * KA, 64)
    b_full[pl.ds(zero_at, 64), :] = jnp.zeros((64, half), jnp.bfloat16)
    rows_x[...] = jnp.zeros_like(rows_x)
    loads[4].wait()
    loads[5].wait()
    for b in range(2 * NX):
        cols = slice(128 * b, 128 * b + 128)
        den = e_v[:, cols] + DAMPING
        num = q_v[:, :, cols].astype(jnp.float32)
        p_send[b] = (num / den[None]).astype(jnp.bfloat16)
    p_full[2 * x + c] = p_send[4 * c + x]

    loads[2].wait()
    for k in far_x:
        arrived(x_recv.at[(x + NX - k) % NX, :, pl.ds(kx, kgx)], "x", (1, k))
    for zz in range(nz):
        gs = kx + 2 * KG * zz
        z_send_g[zz] = jnp.concatenate(
            [x_recv[i, :, gs : gs + 2 * KG] for i in range(NX)], axis=0
        )
    for k in far_z:
        zz = (z + k) % nz
        send(z_send_g.at[zz], tok_g.at[z, c], "z", (1, k), at(x, zz, c))
    send(z_send_g.at[z], tok_g.at[z, c], "c", (1, 0), twin)
    tok_g[z, c] = z_send_g[z]
    loads[3].wait()
    for k in far_x:
        arrived(x_recv.at[(x + NX - k) % NX, :, pl.ds(0, kx)], "x", (0, k))
    for zz in range(nz):
        start = 896 * (zz // 2) + 384 * (zz % 2)
        z_send_a[zz] = jnp.concatenate(
            [x_recv[i, :, start : start + WIN] for i in range(NX)], axis=0
        )
    for k in far_z:
        zz = (z + k) % nz
        send(z_send_a.at[zz], tok_a.at[z, c], "z", (0, k), at(x, zz, c))
    send(z_send_a.at[z], tok_a.at[z, c], "c", (0, 0), twin)
    tok_a[z, c] = z_send_a[z]

    for k in far_s:

        @pl.when(sec >= k)
        def _(k=k):
            pl.semaphore_signal(ready, inc=1, device_id=(sec - k, dp), device_id_type=MESH)

    loads[6].wait()
    loads[7].wait()
    arrived(w_full.at[pl.ds(goff_twin, KG), :], "bw", (1,))
    w_t[...] = w_full[...].astype(jnp.float32).T.astype(jnp.bfloat16)
    arrived(b_full.at[pl.ds(off_twin, KA), :], "bw", (0,))

    tokens = nz * tz

    def forward(tok, kind, k):
        zz = (z + nz - k) % nz
        arrived(tok.at[zz, c], "z", (kind, k))
        send(tok.at[zz, c], tok.at[zz, c], "c", (kind, k), twin)

    def project_acts(k):
        zz = (z + nz - k) % nz
        arrived(tok_a.at[zz, 1 - c], "c", (0, k))
        part = jnp.dot(
            tok_a[zz].reshape(tz, WIN), b_full[...], preferred_element_type=jnp.float32
        ).astype(jnp.bfloat16)
        for i in range(NX):
            xs_a[zz, i] = part[:, 128 * i : 128 * i + 128]
        for kx_ in far_x:
            xx = (x + kx_) % NX
            send(xs_a.at[zz, xx], xr_a.at[zz, x], "rx", (0, k, kx_), at(xx, z, c))

    def project_grads():
        for k in near_z:
            forward(tok_g, 1, k)
        for k in [0] + near_z:
            arrived(tok_g.at[(z + nz - k) % nz, 1 - c], "c", (1, k))
        part = lax.dot_general(
            w_t[...],
            tok_g[...].reshape(tokens, 2 * KG),
            (((1,), (1,)), ((), ())),
            preferred_element_type=jnp.float32,
        ).astype(jnp.bfloat16)
        for i in range(NX):
            for zz in range(nz):
                r = (i // 2) * 2 * nz * ib + zz * 2 * ib + (i % 2) * ib
                xs_g[zz, i] = part[r : r + ib, :]
        for k in far_z + [0]:
            zz = (z + k) % nz
            for kx_ in far_x:
                xx = (x + kx_) % NX
                send(xs_g.at[zz, xx], xr_g.at[zz, x], "rx", (1, k, kx_), at(xx, z, c))

    def sum_over_x(sent, recv, out, kind, k, zz):
        total = sent[zz, x].astype(jnp.float32)
        for kx_ in far_x:
            xx = (x + NX - kx_) % NX
            arrived(recv.at[zz, xx], "rx", (kind, k, kx_))
            total = total + recv[zz, xx].astype(jnp.float32)
        out[zz] = total.astype(jnp.bfloat16)

    def sum_over_z(sums, recv, kind):
        total = sums[z].astype(jnp.float32)
        for k in near_z:
            zz = (z + nz - k) % nz
            arrived(recv.at[zz], "rz", (kind, k))
            total = total + recv[zz].astype(jnp.float32)
        return total.astype(jnp.bfloat16)

    order = [0] + near_z
    split = min(3, nz - 1)
    for i, k in enumerate(order):
        if i == split:
            project_grads()
        if k:
            forward(tok_a, 0, k)
        if i:
            project_acts(order[i - 1])
    project_acts(order[-1])
    for i, (dx, dc) in enumerate(group):
        xx, cc = (x + dx) % NX, (c + dc) % 2
        send(p_send.at[4 * cc + xx], p_full.at[2 * x + c], "p", (i,), at(xx, z, cc))

    for k in far_z + [0]:
        zz = (z + k) % nz
        sum_over_x(xs_g, xr_g, zs_g, 1, k, zz)
        if k:
            send(zs_g.at[zz], zr_g.at[z], "rz", (1, k), at(x, zz, c))
    for k in order:
        zz = (z + nz - k) % nz
        sum_over_x(xs_a, xr_a, zs_a, 0, k, zz)
        if k:
            send(zs_a.at[zz], zr_a.at[z], "rz", (0, nz - k), at(x, zz, c))
    own = sum_over_z(zs_g, zr_g, 1)
    gp_own[...] = own
    for i, (dx, dc) in enumerate(group):
        xx, cc = (x + dx) % NX, (c + dc) % 2
        send(gp_own, gp_full.at[4 * c + x], "gx", (i,), at(xx, z, cc))
    gp_full[4 * c + x] = own
    own = sum_over_z(zs_a, zr_a, 0)
    ap_own[...] = own
    for k in far_z:
        send(ap_own, ap_full.at[z], "az", (k,), at(x, (z + k) % nz, c))
    ap_full[z] = own

    for i, (dx, dc) in enumerate(group):
        xx, cc = (x + NX - dx) % NX, (c + 2 - dc) % 2
        arrived(p_full.at[2 * xx + cc], "p", (i,))
        arrived(gp_full.at[4 * cc + xx], "gx", (i,))
    for k in near_z:
        arrived(ap_full.at[(z + nz - k) % nz], "az", (k,))
    for load in loads[8:]:
        load.wait()
    lane = lax.broadcasted_iota(jnp.int32, (8 * ib, tokens), 1)
    micro = lane % 4
    slot = ((lane // 4) % 4) * 2 * nz + (lane // tz) * 2 + (lane // 16) % 2
    gp = gp_full[...].reshape(8 * ib, tokens).astype(jnp.float32)
    ap = ap_full[...].reshape(tokens, 128)
    for m in range(4):
        live = jnp.where(micro == m, slot, 2**20) < len_ref[m]
        seq = jnp.dot(
            jnp.where(live, gp, 0.0).astype(jnp.bfloat16), ap, preferred_element_type=jnp.float32
        )
        for q in range(8):
            row = seq * p_full[:, q].reshape(8 * ib, 128).astype(jnp.float32)
            rows_x[m * 8 + q : m * 8 + q + 1, :] = jnp.sum(row, axis=0, keepdims=True)
    score = lax.dot_general(
        jnp.ones((8, 128), jnp.float32),
        rows_x[...],
        (((1,), (1,)), ((), ())),
        precision=HIGH,
        preferred_element_type=jnp.float32,
    )
    s1_send[...] = score[0:1, :]
    for i, (dx, dc) in enumerate(group):
        xx, cc = (x + dx) % NX, (c + dc) % 2
        send(s1_send, s1_recv.at[i], "s1", (i,), at(xx, z, cc))
    acc = score[0:1, :]
    for i in range(len(group)):
        arrived(s1_recv.at[i], "s1", (i,))
        acc = acc + s1_recv[i]
    s2_send[...] = acc
    for k in far_z:
        send(s2_send, s2_recv.at[k], "s2", (k,), at(x, (z + k) % nz, c))
    for k in near_z:
        arrived(s2_recv.at[k], "s2", (k,))
        acc = acc + s2_recv[k]
    s3_send[...] = acc

    def score_copy(k):
        return copy_of(s3_send, s3_recv.at[k], "s3", (k,), ((sec + k) % n_sections, dp))


    @pl.when(sec < n_sections - 1)
    def _():
        pl.semaphore_wait(ready, n_sections - 1 - sec)

    for k in far_s:

        @pl.when(sec + k < n_sections)
        def _(k=k):
            score_copy(k).start()

    for k in reversed(far_s):

        @pl.when(sec >= k)
        def _(k=k):
            score_copy(k).wait_recv()

        acc = acc + jnp.where(sec >= k, s3_recv[k], 0.0)

    lane = lax.broadcasted_iota(jnp.int32, (8, 128), 1)
    row = lax.broadcasted_iota(jnp.int32, (8, 128), 0) + dp * 8
    length = jnp.full((8, 128), 1, jnp.int32)
    target = jnp.full((8, 128), -1, jnp.int32)
    for m in range(4):
        inside = lane // 8 == m
        length = jnp.where(inside, len_ref[m], length)
        target = jnp.where(inside, rows_ref[m], target)
    scaled = acc * (1.0 / length.astype(jnp.float32))
    spread = jnp.where(target == row, scaled, 0.0)
    pick = lax.broadcasted_iota(jnp.int32, (128, 128), 0) % 8
    pick = pick == lax.broadcasted_iota(jnp.int32, (128, 128), 1)
    table = jnp.dot(
        spread, pick.astype(jnp.float32), precision=HIGH, preferred_element_type=jnp.float32
    )
    out_ref[...] = prior_ref[...] + table[:, 0:8]
    for copy in pending:
        copy.wait_send()
    for k in far_s:

        @pl.when(sec + k < n_sections)
        def _(k=k):
            score_copy(k).wait_send()


def per_device(n_sections, nz, acts, grads, basis_in, basis_out, eig, query, lengths, rows, prior):
    ff, d = acts.shape[3], grads.shape[3]
    rank = basis_in.shape[2]
    half = rank // 2
    ib = eig.shape[1]
    tokens = 2 * nz * 16
    tz = tokens // nz
    kx, kgx = ff // NX, d // NX
    bf, f32 = jnp.bfloat16, jnp.float32
    dma = pltpu.SemaphoreType.DMA
    vm = pltpu.VMEM
    hbm = pl.BlockSpec(memory_space=pl.ANY)
    vmem = pl.BlockSpec(memory_space=pltpu.VMEM)
    out = pl.pallas_call(
        functools.partial(kernel, n_sections, nz),
        out_shape=jax.ShapeDtypeStruct(prior.shape, f32),
        in_specs=[hbm] * 9,
        out_specs=vmem,
        scratch_shapes=[
            pltpu.SMEM((4,), jnp.int32),
            pltpu.SMEM((4,), jnp.int32),
            vm(prior.shape, f32),
            vm((4, ff), bf),
            vm((4, d), bf),
            vm((ib, rank), f32),
            vm((8, ib, rank), bf),
            vm((WIN, half), bf),
            vm((2 * KG, half), bf),
            vm((half, 2 * KG), bf),
            vm((2 * NX, 8, ib, 128), bf),
            vm((2 * NX, 8, ib, 128), bf),
            vm((NX, 4, kx + kgx), bf),
            vm((nz, 16, WIN), bf),
            vm((nz, 16, 2 * KG), bf),
            vm((nz, 2, 16, WIN), bf),
            vm((nz, 2, 16, 2 * KG), bf),
            vm((nz, NX, tz, 128), bf),
            vm((nz, NX, ib, tokens), bf),
            vm((nz, NX, tz, 128), bf),
            vm((nz, NX, ib, tokens), bf),
            vm((nz, tz, 128), bf),
            vm((nz, ib, tokens), bf),
            vm((nz, tz, 128), bf),
            vm((nz, ib, tokens), bf),
            vm((tz, 128), bf),
            vm((ib, tokens), bf),
            vm((nz, tz, 128), bf),
            vm((2 * NX, ib, tokens), bf),
            vm((128, 128), f32),
            vm((1, 128), f32),
            vm((2 * NX, 1, 128), f32),
            vm((1, 128), f32),
            vm((nz, 1, 128), f32),
            vm((1, 128), f32),
            vm((n_sections, 1, 128), f32),
            dma((11,)),
            pltpu.SemaphoreType.REGULAR,
            dma((2, 2, NX)),
            dma((2, 2, nz)),
            dma((2, 2, nz)),
            dma((2, 2)),
            dma((2, 7)),
            dma((2, 2, nz, NX)),
            dma((2, 2, nz)),
            dma((2, nz)),
            dma((2, 7)),
            dma((2, 7)),
            dma((2, nz)),
            dma((2, n_sections)),
        ],
        compiler_params=pltpu.CompilerParams(collective_id=0, has_side_effects=True),
    )(
        acts.reshape(4, ff),
        grads.reshape(4, d),
        basis_in[0],
        basis_out[0],
        eig[0],
        query[0],
        lengths,
        rows,
        prior,
    )
    return out[None]


def solution(mesh):
    n_sections, n_dp = mesh.shape["section"], mesh.shape["dp"]
    return jax.shard_map(
        functools.partial(per_device, n_sections, n_dp // (NX * NC)),
        mesh=mesh,
        in_specs=(
            P("section", None, "dp", None),
            P("section", None, "dp", None),
            P("section", "dp", None),
            P("section", "dp", None),
            P("section", "dp", None),
            P("section", None, "dp", None),
            P(),
            P(),
            P("dp", None),
        ),
        out_specs=P("section", "dp", None),
        check_vma=False,
    )
```

time: 60.1 us -> 57.8 us (0.962)
  the two profiles are of different devices: /device:TPU:2 before, /device:TPU:56 now
where the time goes in v2:
time: 57.8 us; the launch traced here: 57.6 us
  Pallas kernels  56.3 us (97%)
  local copies, waits for them, and re-layouts  1.28 us (2%)
    pallas_call x1, Pallas kernels, per_device(): pl.pallas_call(functools.partial(kernel, n_sections, nz), out_shape=jax.S...  56.3 us
    unnamed x1, local copies, waits for them, and re-layouts  1.28 us

profile of v2, /device:TPU:56, one launch (start us, length us, event | category | flops | bytes accessed | tf_op | source)
XLA Modules:
  0.0 57.6 jit_solution(2260364057425228251)
XLA Ops:
  0.0 56.3 %shard_map.91 = f32[8,8]{1,0:T(8,128)} custom-call(bf16[4,14336]{1,0:T(4,128)(2,1)} %bitcast.10, bf16[4,4096]{1,0:T(4,128)(2,1)} %bitcast.12, bf16[224,1024]{1,0:T(8,128)(2,1)} %bitcast.7, bf16[64,1024]{1,0:T(8,128)(2,1)} %bitcast.9, f32[16,1024]{1,0:T(8,128)} %bitcast.11, bf16[8,16,1024]{2,1,0:T(8,128)(2,1)} %bitcast.8, s32[4]{0:T(128)} %len_hbm.1, ...), custom_call_target="tpu_custom_call" | custom-call | tf_op jit(solution)/shard_map/pallas_call | solution.py:431
  56.3 1.3 %copy.11 = f32[1,8,8]{2,1,0:T(8,128)} copy(f32[1,8,8]{2,1,0:T(8,128)} %bitcast.13) | data formatting | bytes 512

commit v3 on v2

--- a/solution.py
+++ b/solution.py
@@ -14,7 +14,7 @@
 KA = 224
 KG = 64
 WIN = 512
-SEMS = ("x", "z", "c", "bw", "p", "rx", "rz", "az", "gx", "s1", "s2", "s3")
+SEMS = ("x", "z", "c", "bw", "p", "hx", "rx", "rz", "az", "gx", "s1", "s2", "s3")
 HIGH = lax.Precision.HIGHEST
 
 
@@ -54,6 +54,8 @@
     tok_g,
     xs_a,
     xs_g,
+    xh_a,
+    xh_g,
     xr_a,
     xr_g,
     zs_a,
@@ -247,9 +249,18 @@
         ).astype(jnp.bfloat16)
         for i in range(NX):
             xs_a[zz, i] = part[:, 128 * i : 128 * i + 128]
-        for kx_ in far_x:
-            xx = (x + kx_) % NX
-            send(xs_a.at[zz, xx], xr_a.at[zz, x], "rx", (0, k, kx_), at(xx, z, c))
+        h = tz // 2
+        send(xs_a.at[zz, facing, 0:h], xh_a.at[zz, 0], "hx", (0, k, 0), at(right, z, c))
+        send(xs_a.at[zz, facing, h:tz], xh_a.at[zz, 1], "hx", (0, k, 1), at(left, z, c))
+
+    def relay_acts(k):
+        zz = (z + nz - k) % nz
+        h = tz // 2
+        for side, xx, rows in ((0, right, slice(0, h)), (1, left, slice(h, tz))):
+            arrived(xh_a.at[zz, side], "hx", (0, k, side))
+            both = xs_a[zz, xx, rows].astype(jnp.float32) + xh_a[zz, side].astype(jnp.float32)
+            xs_a[zz, xx, rows] = both.astype(jnp.bfloat16)
+            send(xs_a.at[zz, xx], xr_a.at[zz, side], "rx", (0, k, side), at(xx, z, c))
 
     def project_grads():
         for k in near_z:
@@ -265,20 +276,18 @@
         for i in range(NX):
             for zz in range(nz):
                 r = (i // 2) * 2 * nz * ib + zz * 2 * ib + (i % 2) * ib
-                xs_g[zz, i] = part[r : r + ib, :]
-        for k in far_z + [0]:
-            zz = (z + k) % nz
-            for kx_ in far_x:
-                xx = (x + kx_) % NX
-                send(xs_g.at[zz, xx], xr_g.at[zz, x], "rx", (1, k, kx_), at(xx, z, c))
-
-    def sum_over_x(sent, recv, out, kind, k, zz):
-        total = sent[zz, x].astype(jnp.float32)
-        for kx_ in far_x:
-            xx = (x + NX - kx_) % NX
-            arrived(recv.at[zz, xx], "rx", (kind, k, kx_))
-            total = total + recv[zz, xx].astype(jnp.float32)
-        out[zz] = total.astype(jnp.bfloat16)
+                xs_g[i, zz] = part[r : r + ib, :]
+        h = nz // 2
+        send(xs_g.at[facing, 0:h], xh_g.at[0], "hx", (1, 0, 0), at(right, z, c))
+        send(xs_g.at[facing, h:nz], xh_g.at[1], "hx", (1, 0, 1), at(left, z, c))
+
+    def relay_grads():
+        h = nz // 2
+        for side, xx, rows in ((0, right, slice(0, h)), (1, left, slice(h, nz))):
+            arrived(xh_g.at[side], "hx", (1, 0, side))
+            both = xs_g[xx, rows].astype(jnp.float32) + xh_g[side].astype(jnp.float32)
+            xs_g[xx, rows] = both.astype(jnp.bfloat16)
+            send(xs_g.at[xx], xr_g.at[side], "rx", (1, 0, side), at(xx, z, c))
 
     def sum_over_z(sums, recv, kind):
         total = sums[z].astype(jnp.float32)
@@ -288,6 +297,7 @@
             total = total + recv[zz].astype(jnp.float32)
         return total.astype(jnp.bfloat16)
 
+    right, facing, left = (x + 1) % NX, (x + 2) % NX, (x + 3) % NX
     order = [0] + near_z
     split = min(3, nz - 1)
     for i, k in enumerate(order):
@@ -297,19 +307,31 @@
             forward(tok_a, 0, k)
         if i:
             project_acts(order[i - 1])
+        if i >= 4:
+            relay_acts(order[i - 4])
     project_acts(order[-1])
+    relay_grads()
+    for k in order[max(nz - 4, 0) :]:
+        relay_acts(k)
     for i, (dx, dc) in enumerate(group):
         xx, cc = (x + dx) % NX, (c + dc) % 2
         send(p_send.at[4 * cc + xx], p_full.at[2 * x + c], "p", (i,), at(xx, z, cc))
 
-    for k in far_z + [0]:
+    total = xs_g[x].astype(jnp.float32)
+    for side in (0, 1):
+        arrived(xr_g.at[side], "rx", (1, 0, side))
+        total = total + xr_g[side].astype(jnp.float32)
+    zs_g[...] = total.astype(jnp.bfloat16)
+    for k in far_z:
         zz = (z + k) % nz
-        sum_over_x(xs_g, xr_g, zs_g, 1, k, zz)
-        if k:
-            send(zs_g.at[zz], zr_g.at[z], "rz", (1, k), at(x, zz, c))
+        send(zs_g.at[zz], zr_g.at[z], "rz", (1, k), at(x, zz, c))
     for k in order:
         zz = (z + nz - k) % nz
-        sum_over_x(xs_a, xr_a, zs_a, 0, k, zz)
+        total = xs_a[zz, x].astype(jnp.float32)
+        for side in (0, 1):
+            arrived(xr_a.at[zz, side], "rx", (0, k, side))
+            total = total + xr_a[zz, side].astype(jnp.float32)
+        zs_a[zz] = total.astype(jnp.bfloat16)
         if k:
             send(zs_a.at[zz], zr_a.at[z], "rz", (0, nz - k), at(x, zz, c))
     own = sum_over_z(zs_g, zr_g, 1)
@@ -452,9 +474,11 @@
             vm((nz, 2, 16, WIN), bf),
             vm((nz, 2, 16, 2 * KG), bf),
             vm((nz, NX, tz, 128), bf),
-            vm((nz, NX, ib, tokens), bf),
-            vm((nz, NX, tz, 128), bf),
-            vm((nz, NX, ib, tokens), bf),
+            vm((NX, nz, ib, tokens), bf),
+            vm((nz, 2, tz // 2, 128), bf),
+            vm((2, nz // 2, ib, tokens), bf),
+            vm((nz, 2, tz, 128), bf),
+            vm((2, nz, ib, tokens), bf),
             vm((nz, tz, 128), bf),
             vm((nz, ib, tokens), bf),
             vm((nz, tz, 128), bf),
@@ -477,7 +501,8 @@
             dma((2, 2, nz)),
             dma((2, 2)),
             dma((2, 7)),
-            dma((2, 2, nz, NX)),
+            dma((2, 2, nz, 2)),
+            dma((2, 2, nz, 2)),
             dma((2, 2, nz)),
             dma((2, nz)),
             dma((2, 7)),

time: 57.8 us -> 61 us (1.055)
  Pallas kernels: 56.3 us -> 59.6 us
    pallas_call x1, Pallas kernels: 56.3 us -> 59.6 us  [per_device(): pl.pallas_call(functools.partial(kernel, n_sections, nz), out_shape=jax.S...]
where the time goes in v3:
time: 61 us; the launch traced here: 60.9 us
  Pallas kernels  59.6 us (98%)
  local copies, waits for them, and re-layouts  1.28 us (2%)
    pallas_call x1, Pallas kernels, per_device(): pl.pallas_call(functools.partial(kernel, n_sections, nz), out_shape=jax.S...  59.6 us
    unnamed x1, local copies, waits for them, and re-layouts  1.28 us

profile of v3, /device:TPU:56, one launch (start us, length us, event | category | flops | bytes accessed | tf_op | source)
XLA Modules:
  0.0 60.9 jit_solution(2922792302769651463)
XLA Ops:
  0.0 59.6 %shard_map.91 = f32[8,8]{1,0:T(8,128)} custom-call(bf16[4,14336]{1,0:T(4,128)(2,1)} %bitcast.10, bf16[4,4096]{1,0:T(4,128)(2,1)} %bitcast.12, bf16[224,1024]{1,0:T(8,128)(2,1)} %bitcast.7, bf16[64,1024]{1,0:T(8,128)(2,1)} %bitcast.9, f32[16,1024]{1,0:T(8,128)} %bitcast.11, bf16[8,16,1024]{2,1,0:T(8,128)(2,1)} %bitcast.8, s32[4]{0:T(128)} %len_hbm.1, ...), custom_call_target="tpu_custom_call" | custom-call | tf_op jit(solution)/shard_map/pallas_call | solution.py:453
  59.6 1.3 %copy.11 = f32[1,8,8]{2,1,0:T(8,128)} copy(f32[1,8,8]{2,1,0:T(8,128)} %bitcast.13) | data formatting | bytes 512

commit v4 on v2

--- a/solution.py
+++ b/solution.py
@@ -219,6 +219,9 @@
         send(z_send_a.at[zz], tok_a.at[z, c], "z", (0, k), at(x, zz, c))
     send(z_send_a.at[z], tok_a.at[z, c], "c", (0, 0), twin)
     tok_a[z, c] = z_send_a[z]
+    for i, (dx, dc) in enumerate(group):
+        xx, cc = (x + dx) % NX, (c + dc) % 2
+        send(p_send.at[4 * cc + xx], p_full.at[2 * x + c], "p", (i,), at(xx, z, cc))
 
     for k in far_s:
 
@@ -252,8 +255,6 @@
             send(xs_a.at[zz, xx], xr_a.at[zz, x], "rx", (0, k, kx_), at(xx, z, c))
 
     def project_grads():
-        for k in near_z:
-            forward(tok_g, 1, k)
         for k in [0] + near_z:
             arrived(tok_g.at[(z + nz - k) % nz, 1 - c], "c", (1, k))
         part = lax.dot_general(
@@ -289,18 +290,13 @@
         return total.astype(jnp.bfloat16)
 
     order = [0] + near_z
-    split = min(3, nz - 1)
-    for i, k in enumerate(order):
-        if i == split:
-            project_grads()
-        if k:
-            forward(tok_a, 0, k)
-        if i:
-            project_acts(order[i - 1])
-    project_acts(order[-1])
-    for i, (dx, dc) in enumerate(group):
-        xx, cc = (x + dx) % NX, (c + dc) % 2
-        send(p_send.at[4 * cc + xx], p_full.at[2 * x + c], "p", (i,), at(xx, z, cc))
+    for k in near_z:
+        forward(tok_g, 1, k)
+    for k in near_z:
+        forward(tok_a, 0, k)
+    project_grads()
+    for k in order:
+        project_acts(k)
 
     for k in far_z + [0]:
         zz = (z + k) % nz

time: 57.8 us -> 57.2 us (0.990)
  no operation moved by 1% of the time
where the time goes in v4:
time: 57.2 us; the launch traced here: 57.1 us
  Pallas kernels  55.8 us (98%)
  local copies, waits for them, and re-layouts  1.28 us (2%)
    pallas_call x1, Pallas kernels, per_device(): pl.pallas_call(functools.partial(kernel, n_sections, nz), out_shape=jax.S...  55.8 us
    unnamed x1, local copies, waits for them, and re-layouts  1.28 us

profile of v4, /device:TPU:56, one launch (start us, length us, event | category | flops | bytes accessed | tf_op | source)
XLA Modules:
  0.0 57.1 jit_solution(8052908872834130824)
XLA Ops:
  0.0 55.8 %shard_map.91 = f32[8,8]{1,0:T(8,128)} custom-call(bf16[4,14336]{1,0:T(4,128)(2,1)} %bitcast.10, bf16[4,4096]{1,0:T(4,128)(2,1)} %bitcast.12, bf16[224,1024]{1,0:T(8,128)(2,1)} %bitcast.7, bf16[64,1024]{1,0:T(8,128)(2,1)} %bitcast.9, f32[16,1024]{1,0:T(8,128)} %bitcast.11, bf16[8,16,1024]{2,1,0:T(8,128)(2,1)} %bitcast.8, s32[4]{0:T(128)} %len_hbm.1, ...), custom_call_target="tpu_custom_call" | custom-call | tf_op jit(solution)/shard_map/pallas_call | solution.py:427
  55.8 1.3 %copy.11 = f32[1,8,8]{2,1,0:T(8,128)} copy(f32[1,8,8]{2,1,0:T(8,128)} %bitcast.13) | data formatting | bytes 512

commit v5 on v4

--- a/solution.py
+++ b/solution.py
@@ -267,19 +267,17 @@
             for zz in range(nz):
                 r = (i // 2) * 2 * nz * ib + zz * 2 * ib + (i % 2) * ib
                 xs_g[zz, i] = part[r : r + ib, :]
-        for k in far_z + [0]:
+        for k in far_z:
             zz = (z + k) % nz
-            for kx_ in far_x:
-                xx = (x + kx_) % NX
-                send(xs_g.at[zz, xx], xr_g.at[zz, x], "rx", (1, k, kx_), at(xx, z, c))
-
-    def sum_over_x(sent, recv, out, kind, k, zz):
-        total = sent[zz, x].astype(jnp.float32)
+            send(xs_g.at[zz], zr_g.at[z], "rz", (1, k), at(x, zz, c))
+
+    def sum_over_x(own, recv, kind, k):
+        total = own.astype(jnp.float32)
         for kx_ in far_x:
             xx = (x + NX - kx_) % NX
-            arrived(recv.at[zz, xx], "rx", (kind, k, kx_))
-            total = total + recv[zz, xx].astype(jnp.float32)
-        out[zz] = total.astype(jnp.bfloat16)
+            arrived(recv.at[xx], "rx", (kind, k, kx_))
+            total = total + recv[xx].astype(jnp.float32)
+        return total.astype(jnp.bfloat16)
 
     def sum_over_z(sums, recv, kind):
         total = sums[z].astype(jnp.float32)
@@ -298,27 +296,26 @@
     for k in order:
         project_acts(k)
 
-    for k in far_z + [0]:
-        zz = (z + k) % nz
-        sum_over_x(xs_g, xr_g, zs_g, 1, k, zz)
-        if k:
-            send(zs_g.at[zz], zr_g.at[z], "rz", (1, k), at(x, zz, c))
     for k in order:
         zz = (z + nz - k) % nz
-        sum_over_x(xs_a, xr_a, zs_a, 0, k, zz)
+        zs_a[zz] = sum_over_x(xs_a[zz, x], xr_a.at[zz], 0, k)
         if k:
             send(zs_a.at[zz], zr_a.at[z], "rz", (0, nz - k), at(x, zz, c))
-    own = sum_over_z(zs_g, zr_g, 1)
+    zs_g[...] = sum_over_z(xs_g, zr_g, 1)
+    for kx_ in far_x:
+        xx = (x + kx_) % NX
+        send(zs_g.at[xx], xr_g.at[x], "rx", (1, 0, kx_), at(xx, z, c))
+    own = sum_over_z(zs_a, zr_a, 0)
+    ap_own[...] = own
+    for k in far_z:
+        send(ap_own, ap_full.at[z], "az", (k,), at(x, (z + k) % nz, c))
+    ap_full[z] = own
+    own = sum_over_x(zs_g[x], xr_g, 1, 0)
     gp_own[...] = own
     for i, (dx, dc) in enumerate(group):
         xx, cc = (x + dx) % NX, (c + dc) % 2
         send(gp_own, gp_full.at[4 * c + x], "gx", (i,), at(xx, z, cc))
     gp_full[4 * c + x] = own
-    own = sum_over_z(zs_a, zr_a, 0)
-    ap_own[...] = own
-    for k in far_z:
-        send(ap_own, ap_full.at[z], "az", (k,), at(x, (z + k) % nz, c))
-    ap_full[z] = own
 
     for i, (dx, dc) in enumerate(group):
         xx, cc = (x + NX - dx) % NX, (c + 2 - dc) % 2
@@ -450,11 +447,11 @@
             vm((nz, NX, tz, 128), bf),
             vm((nz, NX, ib, tokens), bf),
             vm((nz, NX, tz, 128), bf),
+            vm((NX, ib, tokens), bf),
+            vm((nz, tz, 128), bf),
+            vm((NX, ib, tokens), bf),
+            vm((nz, tz, 128), bf),
             vm((nz, NX, ib, tokens), bf),
-            vm((nz, tz, 128), bf),
-            vm((nz, ib, tokens), bf),
-            vm((nz, tz, 128), bf),
-            vm((nz, ib, tokens), bf),
             vm((tz, 128), bf),
             vm((ib, tokens), bf),
             vm((nz, tz, 128), bf),

time: 57.2 us -> 55.1 us (0.963)
  Pallas kernels: 55.8 us -> 53.7 us
    pallas_call x1, Pallas kernels: 55.8 us -> 53.7 us  [per_device(): pl.pallas_call(functools.partial(kernel, n_sections, nz), out_shape=jax.S...]
where the time goes in v5:
time: 55.1 us; the launch traced here: 54.9 us
  Pallas kernels  53.7 us (97%)
  local copies, waits for them, and re-layouts  1.28 us (2%)
    pallas_call x1, Pallas kernels, per_device(): pl.pallas_call(functools.partial(kernel, n_sections, nz), out_shape=jax.S...  53.7 us
    unnamed x1, local copies, waits for them, and re-layouts  1.28 us

profile of v5, /device:TPU:56, one launch (start us, length us, event | category | flops | bytes accessed | tf_op | source)
XLA Modules:
  0.0 54.9 jit_solution(8095742588127364148)
XLA Ops:
  0.0 53.7 %shard_map.91 = f32[8,8]{1,0:T(8,128)} custom-call(bf16[4,14336]{1,0:T(4,128)(2,1)} %bitcast.10, bf16[4,4096]{1,0:T(4,128)(2,1)} %bitcast.12, bf16[224,1024]{1,0:T(8,128)(2,1)} %bitcast.7, bf16[64,1024]{1,0:T(8,128)(2,1)} %bitcast.9, f32[16,1024]{1,0:T(8,128)} %bitcast.11, bf16[8,16,1024]{2,1,0:T(8,128)(2,1)} %bitcast.8, s32[4]{0:T(128)} %len_hbm.1, ...), custom_call_target="tpu_custom_call" | custom-call | tf_op jit(solution)/shard_map/pallas_call | solution.py:424
  53.7 1.3 %copy.11 = f32[1,8,8]{2,1,0:T(8,128)} copy(f32[1,8,8]{2,1,0:T(8,128)} %bitcast.13) | data formatting | bytes 512

commit v6 on v5

--- a/solution.py
+++ b/solution.py
@@ -14,7 +14,7 @@
 KA = 224
 KG = 64
 WIN = 512
-SEMS = ("x", "z", "c", "bw", "p", "rx", "rz", "az", "gx", "s1", "s2", "s3")
+SEMS = ("x", "z", "c", "bw", "p", "rx", "rz", "az", "gx", "s1", "s3", "fin")
 HIGH = lax.Precision.HIGHEST
 
 
@@ -67,10 +67,9 @@
     rows_x,
     s1_send,
     s1_recv,
-    s2_send,
-    s2_recv,
     s3_send,
     s3_recv,
+    acc_ref,
     load_sem,
     ready,
     *sem_refs,
@@ -346,42 +345,63 @@
         preferred_element_type=jnp.float32,
     )
     s1_send[...] = score[0:1, :]
-    for i, (dx, dc) in enumerate(group):
-        xx, cc = (x + dx) % NX, (c + dc) % 2
-        send(s1_send, s1_recv.at[i], "s1", (i,), at(xx, z, cc))
-    acc = score[0:1, :]
-    for i in range(len(group)):
-        arrived(s1_recv.at[i], "s1", (i,))
-        acc = acc + s1_recv[i]
-    s2_send[...] = acc
-    for k in far_z:
-        send(s2_send, s2_recv.at[k], "s2", (k,), at(x, (z + k) % nz, c))
-    for k in near_z:
-        arrived(s2_recv.at[k], "s2", (k,))
-        acc = acc + s2_recv[k]
-    s3_send[...] = acc
+    s1_recv[1, 0] = score[0:1, :]
+    places = [(dz, dx) for dz in far_z + [0] for dx in (2, 1, 3, 0)]
+
+    def part_copy(dz, dx):
+        i = dz * NX + dx
+        dev = at((x + dx) % NX, (z + dz) % nz, 1)
+        return copy_of(s1_send, s1_recv.at[c, i], "s1", (c, i), dev)
+
+    for dz, dx in places[:-1]:
+        copy = part_copy(dz, dx)
+        copy.start()
+        pending.append(copy)
+
+    @pl.when(c == 0)
+    def _():
+        part_copy(0, 0).start()
 
     def score_copy(k):
         return copy_of(s3_send, s3_recv.at[k], "s3", (k,), ((sec + k) % n_sections, dp))
 
+    def twin_copy():
+        return copy_of(acc_ref, acc_ref, "fin", (0,), twin)
 
     @pl.when(sec < n_sections - 1)
     def _():
         pl.semaphore_wait(ready, n_sections - 1 - sec)
 
-    for k in far_s:
-
-        @pl.when(sec + k < n_sections)
-        def _(k=k):
-            score_copy(k).start()
-
-    for k in reversed(far_s):
-
-        @pl.when(sec >= k)
-        def _(k=k):
-            score_copy(k).wait_recv()
-
-        acc = acc + jnp.where(sec >= k, s3_recv[k], 0.0)
+    @pl.when(c == 1)
+    def _():
+        for dz, dx in places[::-1]:
+            i = dz * NX + dx
+            if i:
+                arrived(s1_recv.at[1, i], "s1", (1, i))
+            arrived(s1_recv.at[0, i], "s1", (0, i))
+        acc = jnp.sum(s1_recv[...].reshape(2 * NX * nz, 1, 128), axis=0)
+        s3_send[...] = acc
+        for k in far_s:
+
+            @pl.when(sec + k < n_sections)
+            def _(k=k):
+                score_copy(k).start()
+
+        for k in reversed(far_s):
+
+            @pl.when(sec >= k)
+            def _(k=k):
+                score_copy(k).wait_recv()
+
+            acc = acc + jnp.where(sec >= k, s3_recv[k], 0.0)
+        acc_ref[...] = acc
+        twin_copy().start()
+
+    @pl.when(c == 0)
+    def _():
+        twin_copy().wait_recv()
+
+    acc = acc_ref[...]
 
     lane = lax.broadcasted_iota(jnp.int32, (8, 128), 1)
     row = lax.broadcasted_iota(jnp.int32, (8, 128), 0) + dp * 8
@@ -401,11 +421,19 @@
     out_ref[...] = prior_ref[...] + table[:, 0:8]
     for copy in pending:
         copy.wait_send()
-    for k in far_s:
-
-        @pl.when(sec + k < n_sections)
-        def _(k=k):
-            score_copy(k).wait_send()
+
+    @pl.when(c == 0)
+    def _():
+        part_copy(0, 0).wait_send()
+
+    @pl.when(c == 1)
+    def _():
+        twin_copy().wait_send()
+        for k in far_s:
+
+            @pl.when(sec + k < n_sections)
+            def _(k=k):
+                score_copy(k).wait_send()
 
 
 def per_device(n_sections, nz, acts, grads, basis_in, basis_out, eig, query, lengths, rows, prior):
@@ -458,11 +486,10 @@
             vm((2 * NX, ib, tokens), bf),
             vm((128, 128), f32),
             vm((1, 128), f32),
-            vm((2 * NX, 1, 128), f32),
-            vm((1, 128), f32),
-            vm((nz, 1, 128), f32),
+            vm((2, NX * nz, 1, 128), f32),
             vm((1, 128), f32),
             vm((n_sections, 1, 128), f32),
+            vm((1, 128), f32),
             dma((11,)),
             pltpu.SemaphoreType.REGULAR,
             dma((2, 2, NX)),
@@ -474,9 +501,9 @@
             dma((2, 2, nz)),
             dma((2, nz)),
             dma((2, 7)),
-            dma((2, 7)),
-            dma((2, nz)),
+            dma((2, 2, NX * nz)),
             dma((2, n_sections)),
+            dma((2, 1)),
         ],
         compiler_params=pltpu.CompilerParams(collective_id=0, has_side_effects=True),
     )(

time: 55.1 us -> 53.6 us (0.973)
  Pallas kernels: 53.7 us -> 52.2 us
    pallas_call x1, Pallas kernels: 53.7 us -> 52.2 us  [per_device(): pl.pallas_call(functools.partial(kernel, n_sections, nz), out_shape=jax.S...]
where the time goes in v6:
time: 53.6 us; the launch traced here: 53.4 us
  Pallas kernels  52.2 us (97%)
  local copies, waits for them, and re-layouts  1.28 us (2%)
    pallas_call x1, Pallas kernels, per_device(): pl.pallas_call(functools.partial(kernel, n_sections, nz), out_shape=jax.S...  52.2 us
    unnamed x1, local copies, waits for them, and re-layouts  1.28 us

profile of v6, /device:TPU:56, one launch (start us, length us, event | category | flops | bytes accessed | tf_op | source)
XLA Modules:
  0.0 53.4 jit_solution(11018053121321334257)
XLA Ops:
  0.0 52.2 %shard_map.91 = f32[8,8]{1,0:T(8,128)} custom-call(bf16[4,14336]{1,0:T(4,128)(2,1)} %bitcast.10, bf16[4,4096]{1,0:T(4,128)(2,1)} %bitcast.12, bf16[224,1024]{1,0:T(8,128)(2,1)} %bitcast.7, bf16[64,1024]{1,0:T(8,128)(2,1)} %bitcast.9, f32[16,1024]{1,0:T(8,128)} %bitcast.11, bf16[8,16,1024]{2,1,0:T(8,128)(2,1)} %bitcast.8, s32[4]{0:T(128)} %len_hbm.1, ...), custom_call_target="tpu_custom_call" | custom-call | tf_op jit(solution)/shard_map/pallas_call | solution.py:452
  52.2 1.3 %copy.11 = f32[1,8,8]{2,1,0:T(8,128)} copy(f32[1,8,8]{2,1,0:T(8,128)} %bitcast.13) | data formatting | bytes 512

commit v7 on v6

--- a/solution.py
+++ b/solution.py
@@ -451,7 +451,7 @@
     vmem = pl.BlockSpec(memory_space=pltpu.VMEM)
     out = pl.pallas_call(
         functools.partial(kernel, n_sections, nz),
-        out_shape=jax.ShapeDtypeStruct(prior.shape, f32),
+        out_shape=pltpu.VMEM(prior.shape, f32),
         in_specs=[hbm] * 9,
         out_specs=vmem,
         scratch_shapes=[

time: 53.6 us -> 52.3 us (0.976)
  local copies, waits for them, and re-layouts: 1.28 us -> 0.6 us
  Pallas kernels: 52.2 us -> 51.6 us
    unnamed x1, local copies, waits for them, and re-layouts: 1.28 us -> 0.6 us
    pallas_call x1, Pallas kernels: 52.2 us -> 51.6 us  [per_device(): pl.pallas_call(functools.partial(kernel, n_sections, nz), out_shape=pltpu...]
where the time goes in v7:
time: 52.3 us; the launch traced here: 52.2 us
  Pallas kernels  51.6 us (99%)
  local copies, waits for them, and re-layouts  0.6 us (1%)
    pallas_call x1, Pallas kernels, per_device(): pl.pallas_call(functools.partial(kernel, n_sections, nz), out_shape=pltpu...  51.6 us

profile of v7, /device:TPU:56, one launch (start us, length us, event | category | flops | bytes accessed | tf_op | source)
XLA Modules:
  0.0 52.2 jit_solution(3442818514581015656)
XLA Ops:
  0.0 51.6 %shard_map.91 = f32[8,8]{1,0:T(8,128)S(1)} custom-call(bf16[4,14336]{1,0:T(4,128)(2,1)} %bitcast.11, bf16[4,4096]{1,0:T(4,128)(2,1)} %bitcast.13, bf16[224,1024]{1,0:T(8,128)(2,1)} %bitcast.8, bf16[64,1024]{1,0:T(8,128)(2,1)} %bitcast.10, f32[16,1024]{1,0:T(8,128)} %bitcast.12, bf16[8,16,1024]{2,1,0:T(8,128)(2,1)} %bitcast.9, s32[4]{0:T(128)} %len_hbm.1, ...), custom_call_target="tpu_custom_call" | custom-call | tf_op jit(solution)/shard_map/pallas_call | solution.py:452
  51.6 0.6 %copy.11 = f32[1,8,8]{2,1,0:T(8,128)} copy(f32[1,8,8]{2,1,0:T(8,128)S(1)} %bitcast.7) | data formatting | bytes 512
